TPU v7x, 128 devices: a whole 4x4x4 slice. The times are simulated.
128 devices in a mesh: row: 8 (over x, z_hi), col: 4 (over z_lo, core), depth: 4 (over y).
Axes of the slice: x: 4, y: 4, z: 4 (z_hi: 2, z_lo: 2; z = z_hi * 2 + z_lo), core: 2. Of those that a mesh axis runs over, the one named last changes fastest.
Arguments:
- acts: bfloat16 [8192, 5120], P(('depth', 'col'), 'row'), may hold values from -6 to 6
- grad_out: bfloat16 [8192, 13824], P(('depth', 'row'), 'col'), may hold values from -6 to 6
- weight: bfloat16 [5120, 13824], P('row', 'col'), may hold values from -0.078125 to 0.078125
- master: float32 [5120, 13824], P(('row', 'depth'), 'col'), may hold values from -0.078125 to 0.078125
- moment_one: float32 [5120, 13824], P(('row', 'depth'), 'col'), may hold values from -4 to 4
- moment_two: float32 [5120, 13824], P(('row', 'depth'), 'col'), may hold values from 0.05 to 2
Outputs:
- grad_in: bfloat16 [8192, 5120], P(('depth', 'col'), 'row')
- new_weight: bfloat16 [5120, 13824], P('row', 'col')
- new_master: float32 [5120, 13824], P(('row', 'depth'), 'col')
- new_moment_one: float32 [5120, 13824], P(('row', 'depth'), 'col')
- new_moment_two: float32 [5120, 13824], P(('row', 'depth'), 'col')
All inputs are finite; a program needn't handle non-finite values.
Results may differ from a plain program's by a relative error of at most 0.0035.
Values may be sent and summed in bfloat16 or wider, within the bound.
A program may use at most 128 MiB of HBM per device.

v0:
```python
import math

import jax
import jax.numpy as jnp
from jax import lax
from jax.sharding import PartitionSpec as P

STEP = 10


def in_order(parts, dim):
    dims = list(parts.shape[1:])
    dims[dim] *= parts.shape[0]
    return jnp.moveaxis(parts, 0, dim).reshape(dims)


def from_everyone(array, axis):
    count = lax.axis_size(axis)
    return lax.all_to_all(
        jnp.broadcast_to(array[None], (count, *array.shape)), axis, 0, 0, tiled=True
    )


def gathered_copies(array, axis, dim):
    return in_order(from_everyone(array, axis), dim)


def cut_along(array, dim, count):
    before, after = (array.shape[:dim], array.shape[dim + 1 :])
    return jnp.moveaxis(array.reshape(*before, count, -1, *after), dim, 0)


def sum_at_owner(array, axis, dim):
    parts = cut_along(array, dim, lax.axis_size(axis))
    arrived = lax.all_to_all(parts, axis, split_axis=0, concat_axis=0, tiled=True)
    return arrived.sum(axis=0)


def per_device(acts, grad_out, weight, master, moment_one, moment_two):
    whole_acts = gathered_copies(acts, "col", 0)
    tokens_total = acts.shape[0] * lax.axis_size("col") * lax.axis_size("depth")
    whole_cotangent = lax.all_gather(grad_out, "row", axis=0, tiled=True)
    picked = whole_cotangent
    input_sum = sum_at_owner(
        lax.dot_general(
            picked, weight, (((1,), (1,)), ((), ())), preferred_element_type=jnp.float32
        ),
        "col",
        0,
    )
    picked = whole_acts
    grad_sum = lax.psum_scatter(
        lax.dot_general(
            picked, whole_cotangent, (((0,), (0,)), ((), ())), preferred_element_type=jnp.float32
        ).astype(jnp.bfloat16),
        "depth",
        scatter_dimension=0,
        tiled=True,
    ).astype(jnp.float32)
    grad_in = input_sum.astype(jnp.bfloat16)
    grad = grad_sum * jnp.float32(1.0 / math.sqrt(tokens_total))
    new_moment_one = 0.9 * moment_one + 0.1 * grad
    new_moment_two = 0.95 * moment_two + 0.05 * grad * grad
    first_fix = 1.0 - 0.9**STEP
    second_fix = 1.0 - 0.95**STEP
    update = new_moment_one / first_fix / (jnp.sqrt(new_moment_two / second_fix) + 1e-08)
    new_master = master - 0.01 * (update + 0.1 * master)
    new_weight = lax.all_gather(new_master.astype(jnp.bfloat16), "depth", axis=0, tiled=True)
    return (grad_in, new_weight, new_master, new_moment_one, new_moment_two)


def solution(mesh):
    placed = (
        P(("depth", "col"), "row"),
        P(("depth", "row"), "col"),
        P("row", "col"),
        P(("row", "depth"), "col"),
        P(("row", "depth"), "col"),
        P(("row", "depth"), "col"),
    )
    return jax.shard_map(
        per_device,
        mesh=mesh,
        in_specs=placed,
        out_specs=(
            P(("depth", "col"), "row"),
            P("row", "col"),
            P(("row", "depth"), "col"),
            P(("row", "depth"), "col"),
            P(("row", "depth"), "col"),
        ),
        check_vma=False,
    )
```

profile of v0, /device:TPU:1, one launch (start us, length us, event | category | flops | bytes accessed | tf_op | source)
XLA Modules:
  0.0 352.9 jit_solution(4790569811612537850)
XLA Ops:
  7.2 0.0 copy-start.1
  7.2 0.0 all-gather.3.cloned.1.call-start
  7.2 0.7 all-gather.3.cloned.1.call-update
  7.9 0.0 reduce-scatter.2.cloned.1.call-start
  8.0 0.3 copy-done.1
  8.3 0.2 broadcast_in_dim.2
  8.5 50.5 %all_to_all.10 = bf16[4,512,640]{2,1,0:T(8,128)(2,1)S(1)} all-to-all(bf16[4,512,640]{2,1,0:T(8,128)(2,1)S(1)} %broadcast_in_dim.2), channel_id=1, replica_groups=mesh['row'=8,'col'=4,'depth'=4] {'col'}, dimensions={0} | all-to-all | bytes 5242880 | tf_op jit(solution)/shard_map/all_to_all | solution.py:19
  59.0 131.6 %all-gather.3.cloned.1.call-done = bf16[2048,3456]{1,0:T(8,128)(2,1)} async-done(((bf16[256,3456]{1,0:T(8,128)(2,1)}), bf16[2048,3456]{1,0:T(8,128)(2,1)}) %all-gather.3.cloned.1.call-update) | async-done | bytes 14155792 | tf_op jit(solution)/shard_map/all_gather | solution.py:42
  190.6 14.4 %convolution_convert_fusion = bf16[640,3456]{1,0:T(8,128)(2,1)} fusion(bf16[2048,640]{1,0:T(8,128)(2,1)S(1)} %bitcast.7, bf16[2048,3456]{1,0:T(8,128)(2,1)} %all-gather.3.cloned.1.call-done), kind=kOutput, calls=%fused_computation | convolution fusion | flops 9061908480 | bytes 21200896 | tf_op jit(solution)/shard_map/dot_general | solution.py:53
  205.1 0.0 copy-start
  205.1 0.0 reduce-scatter.2.cloned.1.call-update
  205.1 0.0 all-gather.5.cloned.1.call-start
  205.1 47.2 %reduce-scatter.2.cloned.1.call-done = bf16[160,3456]{1,0:T(8,128)(2,1)} async-done(((bf16[640,3456]{1,0:T(8,128)(2,1)}), bf16[160,3456]{1,0:T(8,128)(2,1)}) %reduce-scatter.2.cloned.1.call-update) | async-done | bytes 1105936 | tf_op jit(solution)/shard_map/reduce_scatter | solution.py:52
  252.3 0.0 copy-done
  252.3 7.0 %fusion.3 = (bf16[160,3456]{1,0:T(8,128)(2,1)}, f32[160,3456]{1,0:T(8,128)}, f32[160,3456]{1,0:T(8,128)}, f32[160,3456]{1,0:T(8,128)}) fusion(f32[160,3456]{1,0:T(8,128)S(1)} %copy-done, bf16[160,3456]{1,0:T(8,128)(2,1)} %reduce-scatter.2.cloned.1.call-done, f32[160,3456]{1,0:T(8,128)} %param.10, f32[160,3456]{1,0:T(8,128)} %param.11), kind=kLoop, calls=%fused_computation.8 | loop fusion | flops 9953280 | bytes 15482880 | tf_op jit(solution)/shard_map/convert_element_type | solution.py:68
  259.4 0.0 all-gather.5.cloned.1.call-update
  259.4 15.9 %fusion.6 = f32[2048,640]{1,0:T(8,128)S(1)} fusion(bf16[2048,3456]{1,0:T(8,128)(2,1)} %all-gather.3.cloned.1.call-done, bf16[640,3456]{1,0:T(8,128)(2,1)} %param.8), kind=kOutput, calls=%fused_computation.9 | convolution fusion | flops 9059696640 | bytes 23822336 | tf_op jit(solution)/shard_map/dot_general | solution.py:45
  275.3 62.6 %all_to_all.11 = f32[4,512,640]{2,1,0:T(8,128)} all-to-all(f32[4,512,640]{2,1,0:T(8,128)S(1)} %bitcast.6), channel_id=1, replica_groups=mesh['row'=8,'col'=4,'depth'=4] {'col'}, dimensions={0} | all-to-all | bytes 10485760 | tf_op jit(solution)/shard_map/all_to_all | solution.py:35
  337.9 3.8 %reduce_sum.9 = bf16[512,640]{1,0:T(8,128)(2,1)} reduce(f32[4,512,640]{2,1,0:T(8,128)} %all_to_all.11, f32[]{:T(128)} %constant.4.clone.1), dimensions={0}, to_apply=%region_0.0 | reduce | flops 983040 | bytes 5898244 | tf_op jit(solution)/shard_map/reduce_sum | solution.py:36
  341.7 0.0 all-gather.5.cloned.1.call-done
  341.7 4.6 %copy.12 = bf16[640,3456]{1,0:T(8,128)(2,1)} copy(bf16[640,3456]{1,0:T(8,128)(2,1)} %all-gather.5.cloned.1.call-done) | data formatting | bytes 8847360
Async XLA Ops:
  7.2 1.1 copy-start.1
  7.2 183.5 %all-gather.3.cloned.1.call-start = ((), (), s32[]{:S(2)}) async-start(), calls=%async_computation.3 | async-start | bytes 15925248 | tf_op jit(solution)/shard_map/all_gather | solution.py:42
  7.9 244.4 %reduce-scatter.2.cloned.1.call-start = ((), (), s32[]{:S(2)}) async-start(), calls=%async_computation.4 | async-start | bytes 5529600 | tf_op jit(solution)/shard_map/reduce_scatter | solution.py:52
  205.1 47.3 %copy-start = (f32[160,3456]{1,0:T(8,128)S(1)}, f32[160,3456]{1,0:T(8,128)}, u32[]{:S(2)}) copy-start(f32[160,3456]{1,0:T(8,128)} %param.9) | copy-start | bytes 6635524
  205.1 136.6 %all-gather.5.cloned.1.call-start = ((), (), s32[]{:S(2)}) async-start(), calls=%async_computation.5 | async-start | bytes 5529600 | tf_op jit(solution)/shard_map/all_gather | solution.py:68
Sparse Core Ops, SparseCore 0:
  10.3 180.2 all-gather.2
  205.2 47.0 reduce-scatter.1
  259.5 49.7 all-gather.4
where the time goes:
time: 353 us
  waiting for transfers between devices  180 us (51%)
  blocking collectives  113 us (32%)
  matrix products  30.3 us (9%)
  between operations  13.8 us (4%)
  other arithmetic  10.8 us (3%)
  local copies, waits for them, and re-layouts  5.15 us (1%)
    all_gather x1, waiting for transfers between devices, per_device(): whole_cotangent = lax.all_gather(grad_out, 'row', axis=0, tiled=True)  132 us
    all_to_all x1, blocking collectives, sum_at_owner(): lax.all_to_all(parts, axis, split_axis=0, concat_axis=0, tiled=True)  62.6 us
    all_to_all x1, blocking collectives, from_everyone(): lax.all_to_all(jnp.broadcast_to(array[None], (count, *array.shape)), axis...  50.5 us
    reduce_scatter x1, waiting for transfers between devices, per_device(): lax.psum_scatter(lax.dot_general(picked, whole_cotangent, (((0,), (0,)),...  47.2 us
    dot_general x1, matrix products, per_device(): lax.dot_general(picked, weight, (((1,), (1,)), ((), ())), preferred_eleme...  15.9 us
    dot_general x1, matrix products, per_device(): lax.dot_general(picked, whole_cotangent, (((0,), (0,)), ((), ())), prefer...  14.4 us
  transfers between devices with their start and end apart: 3, of which 2 were waited for; matrix products, arithmetic and copies ran while one was open for 6% of the time, Pallas kernels for 0%

commit v1 on v0

v1 whole, which is shorter than its diff:
```python
import math

import jax
import jax.numpy as jnp
from jax import lax
from jax.experimental import pallas as pl
from jax.experimental.pallas import tpu as pltpu
from jax.sharding import PartitionSpec as P

STEP = 10
WC = 384
MESH = pl.DeviceIdType.MESH
F32, BF16 = jnp.float32, jnp.bfloat16


def place():
    r, c, d = lax.axis_index("row"), lax.axis_index("col"), lax.axis_index("depth")
    return r // 2, lax.rem(r, 2), c // 2, lax.rem(c, 2), d


def adamw(grad, master, one, two):
    new_one = 0.9 * one + 0.1 * grad
    new_two = 0.95 * two + 0.05 * grad * grad
    first_fix = 1.0 - 0.9**STEP
    second_fix = 1.0 - 0.95**STEP
    update = new_one / first_fix / (jnp.sqrt(new_two / second_fix) + 1e-08)
    return master - 0.01 * (update + 0.1 * master), new_one, new_two


def kernel(
    nc, scale,
    acts, grad_out, weight, master, moment_one, moment_two,
    grad_in, new_weight, new_master, new_one, new_two,
    G, W, ACT, AT, GI, D2D, SB, RB, GO, GS, RS, OPT, NW,
    g_sem, w_sem, a_sem, o_sem, out_sem, nw_sem, gi_sem,
    ts, tr, acs, acr, rss, rsr, ags, agr, ds, dr, zs, zr,
):
    x, h, zl, k, d = place()
    me = x * 2 + h
    col = zl * 2 + k
    xr, xl = lax.rem(x + 1, 4), lax.rem(x + 3, 4)
    left, right = xl * 2 + h, xr * 2 + h
    anti = lax.rem(x + 2, 4) * 2 + h
    zpart = x * 2 + (1 - h)
    dup, ddn, dan = lax.rem(d + 1, 4), lax.rem(d + 3, 4), lax.rem(d + 2, 4)

    d_right, d_left = (right, col, d), (left, col, d)
    d_zp = (zpart, col, d)
    d_core = (me, zl * 2 + (1 - k), d)
    d_zl = (me, (1 - zl) * 2 + k, d)
    d_up, d_dn, d_an = (me, col, dup), (me, col, ddn), (me, col, dan)

    def cols(c):
        return pl.ds(pl.multiple_of(c * WC, WC), WC)

    def load_g(c):
        return pltpu.make_async_copy(grad_out.at[:, cols(c)], G.at[c, me], g_sem.at[c])

    def load_w(c):
        return pltpu.make_async_copy(weight.at[:, cols(c)], W.at[c], w_sem.at[c])

    def load_o(c):
        return [
            pltpu.make_async_copy(ref.at[:, cols(c)], OPT.at[c, n], o_sem.at[c, n])
            for n, ref in enumerate((master, moment_one, moment_two))
        ]

    def store_o(c):
        return [
            pltpu.make_async_copy(OPT.at[c, n], ref.at[:, cols(c)], out_sem.at[c, n])
            for n, ref in enumerate((new_master, new_one, new_two))
        ]

    def store_w(c):
        return [
            pltpu.make_async_copy(
                NW.at[c, p], new_weight.at[pl.ds(p * 160, 160), cols(c)], nw_sem.at[c, p]
            )
            for p in range(4)
        ]

    load_a = pltpu.make_async_copy(acts, ACT.at[col], a_sem.at[0])

    load_g(0).start()
    load_a.start()
    load_g(1).start()

    barrier = pltpu.get_barrier_semaphore()
    for peer in (d_right, d_left, d_zp, d_core, d_zl, d_up, d_dn, d_an):
        pl.semaphore_signal(barrier, inc=1, device_id=peer, device_id_type=MESH)

    @pl.loop(2, nc)
    def _(c):
        load_g(c).start()

    @pl.loop(0, nc)
    def _(c):
        load_w(c).start()

    @pl.loop(0, nc)
    def _(c):
        for copy in load_o(c):
            copy.start()

    pl.semaphore_wait(barrier, 8)

    LO, HI, ALL = pl.ds(0, 128), pl.ds(128, 128), pl.ds(0, 256)

    def flow(n, c):
        slot, rows, peer = (
            (me, ALL, d_right), (me, ALL, d_left), (me, ALL, d_zp),
            (left, LO, d_right), (right, HI, d_left),
            (zpart, ALL, d_right), (zpart, ALL, d_left),
            (anti, LO, d_zp), (anti, HI, d_zp),
        )[n]
        ref = G.at[c, slot, rows]
        return pltpu.make_async_remote_copy(
            ref, ref, ts.at[c, n], tr.at[c, n], device_id=peer, device_id_type=MESH
        )

    def arrived(n, c):
        flow(n, c).wait_recv()

    def act_flow(n):
        slot, peer = ((col, d_zl), (col, d_core), ((1 - zl) * 2 + k, d_core))[n]
        ref = ACT.at[slot]
        return pltpu.make_async_remote_copy(
            ref, ref, acs.at[n], acr.at[n], device_id=peer, device_id_type=MESH
        )

    def rs_flow(n, c):
        piece, peer = ((dup, d_up), (dan, d_an), (ddn, d_dn))[n]
        return pltpu.make_async_remote_copy(
            GS.at[c, piece], RS.at[c, n], rss.at[c, n], rsr.at[c, n],
            device_id=peer, device_id_type=MESH,
        )

    def ag_flow(n, c):
        piece, rows, peer = (
            (d, pl.ds(0, 160), d_up), (d, pl.ds(0, 160), d_dn),
            (ddn, pl.ds(0, 80), d_up), (dup, pl.ds(80, 80), d_dn),
        )[n]
        ref = NW.at[c, piece, rows]
        return pltpu.make_async_remote_copy(
            ref, ref, ags.at[c, n], agr.at[c, n], device_id=peer, device_id_type=MESH
        )

    def core_flow(n):
        return pltpu.make_async_remote_copy(
            GI.at[n * 2 + (1 - k)], D2D.at[n], ds.at[n], dr.at[n],
            device_id=d_core, device_id_type=MESH,
        )

    zl_flow = pltpu.make_async_remote_copy(
        SB, RB, zs.at[0], zr.at[0], device_id=d_zl, device_id_type=MESH
    )

    def own_sends(c):
        load_g(c).wait()
        flow(2, c).start()
        flow(0, c).start()
        flow(1, c).start()

    own_sends(0)
    load_a.wait()
    act_flow(0).start()
    act_flow(1).start()
    own_sends(1)

    GI[...] = jnp.zeros_like(GI)

    def turn_acts(slot):
        AT[:, pl.ds(pl.multiple_of(slot * 512, 512), 512)] = ACT[slot].T

    def input_sums(c):
        @pl.loop(0, 4)
        def _(o):
            g = G[c, pl.ds(o * 2, 2)].reshape(512, WC)
            GI[o] += lax.dot_general(
                g, W[c], (((1,), (1,)), ((), ())), preferred_element_type=F32
            )

    def weight_grad(c):
        g = G[c].reshape(2048, WC)

        @pl.loop(0, 4)
        def _(p):
            rows = AT[pl.ds(pl.multiple_of(p * 160, 160), 160), :]
            GS[c, p] = jnp.dot(rows, g, preferred_element_type=F32).astype(BF16)

    @pl.loop(0, nc + 5)
    def _(i):
        @pl.when(i + 2 < nc)
        def _():
            own_sends(i + 2)

        @pl.when(i < nc)
        def _():
            arrived(2, i)
            flow(5, i).start()
            flow(6, i).start()
            arrived(0, i)
            flow(3, i).start()
            arrived(1, i)
            flow(4, i).start()

        @pl.when((i >= 1) & (i < nc + 1))
        def _():
            arrived(3, i - 1)
            flow(7, i - 1).start()
            arrived(4, i - 1)
            flow(8, i - 1).start()

        @pl.when(i == 1)
        def _():
            turn_acts(col)
            act_flow(1).wait_recv()
            turn_acts(zl * 2 + (1 - k))
            act_flow(0).wait_recv()
            act_flow(2).start()
            turn_acts((1 - zl) * 2 + k)

        @pl.when(i == 2)
        def _():
            act_flow(2).wait_recv()
            turn_acts((1 - zl) * 2 + (1 - k))

        @pl.when((i >= 2) & (i < nc + 2))
        def _():
            c = i - 2
            for n in (5, 6, 7, 8):
                arrived(n, c)
            load_w(c).wait()

            input_sums(c)

            @pl.when(c == nc - 1)
            def _():
                core_flow(0).start()
                core_flow(1).start()

            weight_grad(c)
            for n in range(3):
                rs_flow(n, c).start()

            @pl.when(c == nc - 1)
            def _():
                core_flow(0).wait_recv()
                core_flow(1).wait_recv()
                SB[...] = (GI[(1 - zl) * 2 + k] + D2D[1 - zl]).astype(BF16)
                zl_flow.start()

        @pl.when((i >= 3) & (i < nc + 3))
        def _():
            c = i - 3
            for n in range(3):
                rs_flow(n, c).wait_recv()
            for copy in load_o(c):
                copy.wait()
            grad = GS[c, d].astype(F32)
            for n in range(3):
                grad = grad + RS[c, n].astype(F32)
            a, b, e = adamw(grad * scale, OPT[c, 0], OPT[c, 1], OPT[c, 2])
            NW[c, d] = a.astype(BF16)
            OPT[c, 0] = a
            OPT[c, 1] = b
            OPT[c, 2] = e
            ag_flow(0, c).start()
            ag_flow(1, c).start()
            for copy in store_o(c):
                copy.start()

        @pl.when((i >= 4) & (i < nc + 4))
        def _():
            c = i - 4
            ag_flow(0, c).wait_recv()
            ag_flow(2, c).start()
            ag_flow(1, c).wait_recv()
            ag_flow(3, c).start()

        @pl.when(i >= 5)
        def _():
            c = i - 5
            ag_flow(2, c).wait_recv()
            ag_flow(3, c).wait_recv()
            for copy in store_w(c):
                copy.start()

    zl_flow.wait_recv()
    GO[...] = (GI[col] + D2D[zl] + RB[...].astype(F32)).astype(BF16)
    out = pltpu.make_async_copy(GO, grad_in, gi_sem.at[0])
    out.start()

    @pl.loop(0, nc)
    def _(c):
        for n in range(9):
            flow(n, c).wait_send()
        for n in range(3):
            rs_flow(n, c).wait_send()
        for n in range(4):
            ag_flow(n, c).wait_send()
        for copy in store_o(c) + store_w(c):
            copy.wait()

    for n in range(3):
        act_flow(n).wait_send()
    core_flow(0).wait_send()
    core_flow(1).wait_send()
    zl_flow.wait_send()
    out.wait()


def per_device(acts, grad_out, weight, master, moment_one, moment_two):
    tokens_total = acts.shape[0] * lax.axis_size("col") * lax.axis_size("depth")
    width = grad_out.shape[1]
    nc = width // WC
    scale = float(1.0 / math.sqrt(tokens_total))
    dma = pltpu.SemaphoreType.DMA
    anywhere = pl.BlockSpec(memory_space=pl.ANY)

    def body(*refs):
        kernel(nc, scale, *refs)

    return pl.pallas_call(
        body,
        out_shape=(
            jax.ShapeDtypeStruct(acts.shape, BF16),
            jax.ShapeDtypeStruct(weight.shape, BF16),
            jax.ShapeDtypeStruct(master.shape, F32),
            jax.ShapeDtypeStruct(master.shape, F32),
            jax.ShapeDtypeStruct(master.shape, F32),
        ),
        in_specs=[anywhere] * 6,
        out_specs=(anywhere,) * 5,
        scratch_shapes=[
            pltpu.VMEM((nc, 8, 256, WC), BF16),
            pltpu.VMEM((nc, 640, WC), BF16),
            pltpu.VMEM((4, 512, 640), BF16),
            pltpu.VMEM((640, 2048), BF16),
            pltpu.VMEM((4, 512, 640), F32),
            pltpu.VMEM((2, 512, 640), F32),
            pltpu.VMEM((512, 640), BF16),
            pltpu.VMEM((512, 640), BF16),
            pltpu.VMEM((512, 640), BF16),
            pltpu.VMEM((nc, 4, 160, WC), BF16),
            pltpu.VMEM((nc, 3, 160, WC), BF16),
            pltpu.VMEM((nc, 3, 160, WC), F32),
            pltpu.VMEM((nc, 4, 160, WC), BF16),
            dma((nc,)), dma((nc,)), dma((1,)), dma((nc, 3)), dma((nc, 3)), dma((nc, 4)), dma((1,)),
            dma((nc, 9)), dma((nc, 9)),
            dma((3,)), dma((3,)),
            dma((nc, 3)), dma((nc, 3)),
            dma((nc, 4)), dma((nc, 4)),
            dma((2,)), dma((2,)),
            dma((1,)), dma((1,)),
        ],
        compiler_params=pltpu.CompilerParams(
            collective_id=0, has_side_effects=True, vmem_limit_bytes=67_000_000
        ),
        name="step",
    )(acts, grad_out, weight, master, moment_one, moment_two)


def solution(mesh):
    placed = (
        P(("depth", "col"), "row"),
        P(("depth", "row"), "col"),
        P("row", "col"),
        P(("row", "depth"), "col"),
        P(("row", "depth"), "col"),
        P(("row", "depth"), "col"),
    )
    return jax.shard_map(
        per_device,
        mesh=mesh,
        in_specs=placed,
        out_specs=(
            P(("depth", "col"), "row"),
            P("row", "col"),
            P(("row", "depth"), "col"),
            P(("row", "depth"), "col"),
            P(("row", "depth"), "col"),
        ),
        check_vma=False,
    )
```

time: 353 us -> 159 us (0.45)
  waiting for transfers between devices: 180 us -> 0 us
  Pallas kernels: 0 us -> 145 us
  blocking collectives: 113 us -> 0 us
  matrix products: 30.3 us -> 0 us
  between operations: 13.8 us -> 0.65 us
  other arithmetic: 10.8 us -> 0 us
  local copies, waits for them, and re-layouts: 5.15 us -> 13 us
    pallas_call x0 -> x1, Pallas kernels: none -> 145 us  [per_device(): pl.pallas_call(body, out_shape=(jax.ShapeDtypeStruct(acts.shape, BF16), j...]
    all_gather x2 -> x0, waiting for transfers between devices: 132 us -> none  [the longest x1 132 us: per_device(): whole_cotangent = lax.all_gather(grad_out, 'row', axis=0, tiled=True)]
    all_to_all x2 -> x0, blocking collectives: 113 us -> none  [the longest x1 62.6 us: sum_at_owner(): lax.all_to_all(parts, axis, split_axis=0, concat_axis=0, tiled=True)]
    reduce_scatter x1 -> x0, waiting for transfers between devices: 47.2 us -> none  [per_device(): lax.psum_scatter(lax.dot_general(picked, whole_cotangent, (((0,), (0,)),...]
    dot_general x2 -> x0, matrix products: 30.3 us -> none  [the longest x1 15.9 us: per_device(): lax.dot_general(picked, weight, (((1,), (1,)), ((), ())), preferred_eleme...]
    unnamed x5 -> x11, local copies, waits for them, and re-layouts: 4.95 us -> 13 us
    convert_element_type x1 -> x0, other arithmetic: 7.03 us -> none  [per_device(): new_master.astype(jnp.bfloat16)]
    reduce_sum x1 -> x0, other arithmetic: 3.81 us -> none  [sum_at_owner(): return arrived.sum(axis=0)]
  transfers between devices with their start and end apart: 3 -> 0, of which waited for: 2 -> 0; matrix products, arithmetic and copies ran while one was open for 6% -> 0% of each run, Pallas kernels for 0% -> 0%
where the time goes in v1:
time: 159 us
  Pallas kernels  145 us (91%)
  local copies, waits for them, and re-layouts  13 us (8%)
    pallas_call x1, Pallas kernels, per_device(): pl.pallas_call(body, out_shape=(jax.ShapeDtypeStruct(acts.shape, BF16), j...  145 us
    unnamed x11, local copies, waits for them, and re-layouts  13 us

profile of v1, /device:TPU:1, one launch (start us, length us, event | category | flops | bytes accessed | tf_op | source)
XLA Modules:
  0.0 159.0 jit_solution(15600063421939267911)
XLA Ops:
  0.6 145.4 %step.1 = (bf16[512,640]{1,0:T(8,128)(2,1)}, bf16[640,3456]{1,0:T(8,128)(2,1)}, f32[160,3456]{1,0:T(8,128)}, f32[160,3456]{1,0:T(8,128)}, f32[160,3456]{1,0:T(8,128)}) custom-call(bf16[512,640]{1,0:T(8,128)(2,1)} %refs_0_.1, bf16[256,3456]{1,0:T(8,128)(2,1)} %refs_1_.1, bf16[640,3456]{1,0:T(8,128)(2,1)} %refs_2_.1, f32[160,3456]{1,0:T(8,128)} %refs_3_.1, ...), custom_call_target="tpu_custom_call" | custom-call | tf_op jit(solution)/shard_map/step/pallas_call | solution.py:324
  146.1 2.0 %copy.16 = bf16[512,640]{1,0:T(8,128)(2,1)} copy(bf16[512,640]{1,0:T(8,128)(2,1)} %get-tuple-element.10) | data formatting | bytes 1310720
  148.0 0.0 copy-start.2
  148.0 4.8 %copy.17 = bf16[640,3456]{1,0:T(8,128)(2,1)} copy(bf16[640,3456]{1,0:T(8,128)(2,1)} %get-tuple-element.11) | data formatting | bytes 8847360
  152.8 0.0 copy-done.2
  152.8 0.0 copy-start.1
  152.8 1.4 copy.18
  154.2 1.1 copy-done.1
  155.3 0.0 copy-start
  155.3 1.4 copy.19
  156.6 1.1 copy-done
  157.7 1.4 copy.20
Async XLA Ops:
  148.0 4.8 %copy-start.2 = (f32[160,3456]{1,0:T(8,128)S(1)}, f32[160,3456]{1,0:T(8,128)}, u32[]{:S(2)}) copy-start(f32[160,3456]{1,0:T(8,128)} %get-tuple-element.12) | copy-start | bytes 6635524
  152.8 2.4 %copy-start.1 = (f32[160,3456]{1,0:T(8,128)S(1)}, f32[160,3456]{1,0:T(8,128)}, u32[]{:S(2)}) copy-start(f32[160,3456]{1,0:T(8,128)} %get-tuple-element.13) | copy-start | bytes 6635524
  155.3 2.4 %copy-start = (f32[160,3456]{1,0:T(8,128)S(1)}, f32[160,3456]{1,0:T(8,128)}, u32[]{:S(2)}) copy-start(f32[160,3456]{1,0:T(8,128)} %get-tuple-element.14) | copy-start | bytes 6635524

commit v2 on v0

v2 whole, which is shorter than its diff:
```python
import math

import jax
import jax.numpy as jnp
from jax import lax
from jax.experimental import pallas as pl
from jax.experimental.pallas import tpu as pltpu
from jax.sharding import PartitionSpec as P

STEP = 10
BY_X = 2
STRIP = 128
GROUP = 3
WIDE = STRIP * GROUP

MESH = pl.DeviceIdType.MESH
F32, BF16 = jnp.float32, jnp.bfloat16


def place():
    r, c, d = lax.axis_index("row"), lax.axis_index("col"), lax.axis_index("depth")
    return r // 2, lax.rem(r, 2), c // 2, lax.rem(c, 2), d


def adamw(grad, master, one, two):
    new_one = 0.9 * one + 0.1 * grad
    new_two = 0.95 * two + 0.05 * grad * grad
    first_fix = 1.0 - 0.9**STEP
    second_fix = 1.0 - 0.95**STEP
    update = new_one / first_fix / (jnp.sqrt(new_two / second_fix) + 1e-08)
    return master - 0.01 * (update + 0.1 * master), new_one, new_two


def kernel(
    nc, scale,
    acts, grad_out, weight, master, moment_one, moment_two,
    grad_in, new_weight, new_master, new_one, new_two,
    G, W, ACT, AT, GI, D2D, SB, RB, GS, RS,
    g_sem, w_sem, a_sem, o_sem,
    ts, tr, acs, acr, rss, rsr, ags, agr, ds, dr, zs, zr,
):
    x, h, zl, k, d = place()
    me = x * 2 + h
    col = zl * 2 + k
    xr, xl = lax.rem(x + 1, 4), lax.rem(x + 3, 4)
    left, right = xl * 2 + h, xr * 2 + h
    anti = lax.rem(x + 2, 4) * 2 + h
    zpart = x * 2 + (1 - h)
    left_zp, right_zp = xl * 2 + (1 - h), xr * 2 + (1 - h)
    dup, ddn, dan = lax.rem(d + 1, 4), lax.rem(d + 3, 4), lax.rem(d + 2, 4)

    d_right, d_left = (right, col, d), (left, col, d)
    d_zp = (zpart, col, d)
    d_core = (me, zl * 2 + (1 - k), d)
    d_zl = (me, (1 - zl) * 2 + k, d)
    d_up, d_dn = (me, col, dup), (me, col, ddn)

    last = nc - 1

    def strips(q):
        return pl.ds(q * GROUP, GROUP)

    def cols(q):
        return pl.ds(pl.multiple_of(q * WIDE, STRIP), WIDE)

    def load_g(q):
        return [
            pltpu.make_async_copy(
                grad_out.at[:, :, :, pl.ds(pl.multiple_of((q * GROUP + n) * STRIP, STRIP), STRIP)],
                G.at[q * GROUP + n, me],
                g_sem.at[q, n],
            )
            for n in range(GROUP)
        ]

    def load_o(n):
        ref, to = ((master, new_master), (moment_one, new_one), (moment_two, new_two))[n]
        return pltpu.make_async_copy(ref, to, o_sem.at[n])

    load_w = pltpu.make_async_copy(weight, W, w_sem.at[0])
    load_a = pltpu.make_async_copy(acts, ACT.at[col], a_sem.at[0])

    def start_g(q):
        for copy in load_g(q):
            copy.start()

    def loaded_g(q):
        for copy in load_g(q):
            copy.wait()

    start_g(0)
    start_g(1)
    load_a.start()

    barrier = pltpu.get_barrier_semaphore()
    for peer in (d_right, d_left, d_zp, d_core, d_zl, d_up, d_dn):
        pl.semaphore_signal(barrier, inc=1, device_id=peer, device_id_type=MESH)

    @pl.loop(2, nc)
    def _(q):
        start_g(q)

    load_w.start()
    for n in range(3):
        load_o(n).start()

    pl.semaphore_wait(barrier, 7)

    def flow(n, q, piece=None):
        slot, half, peer = (
            (me, None, d_right), (me, None, d_left), (me, None, d_zp),
            (left, 0, d_right), (right, 1, d_left),
            (zpart, None, d_right), (zpart, None, d_left),
            (anti, 0, d_zp), (anti, 1, d_zp),
            (left_zp, 0, d_right), (right_zp, 1, d_left),
        )[n]
        n = n - 2 if n > 8 else n
        ref = G.at[
            strips(q), slot,
            pl.ds(0, 2) if half is None else half,
            pl.ds(0, 2) if piece is None else piece,
        ]
        sem = q if piece is None else last + piece
        return pltpu.make_async_remote_copy(
            ref, ref, ts.at[sem, n], tr.at[sem, n], device_id=peer, device_id_type=MESH
        )

    def arrived(n, q, piece=None):
        flow(n, q, piece).wait_recv()

    def act_flow(n):
        slot, peer = ((col, d_zl), (col, d_core), ((1 - zl) * 2 + k, d_core))[n]
        ref = ACT.at[slot]
        return pltpu.make_async_remote_copy(
            ref, ref, acs.at[n], acr.at[n], device_id=peer, device_id_type=MESH
        )

    TOP, LOW = pl.ds(0, 80), pl.ds(80, 80)

    def rs_flow(n, q):
        piece, rows, slot, peer = (
            (dan, TOP, 2, d_up), (dan, LOW, 2, d_dn),
            (dup, LOW, 0, d_up), (ddn, TOP, 1, d_dn),
            (dup, TOP, 0, d_up), (ddn, LOW, 1, d_dn),
        )[n]
        at = strips(q)
        return pltpu.make_async_remote_copy(
            GS.at[at, piece, rows], RS.at[at, slot, rows], rss.at[q, n], rsr.at[q, n],
            device_id=peer, device_id_type=MESH,
        )

    def ag_flow(n, q):
        piece, first, count, peer = (
            (d, 0, 160, d_up), (d, 0, 160, d_dn), (ddn, 0, 80, d_up), (dup, 80, 80, d_dn),
        )[n]
        rows = pl.ds(pl.multiple_of(piece * 160 + first, 16), count)
        ref = new_weight.at[rows, cols(q)]
        return pltpu.make_async_remote_copy(
            ref, ref, ags.at[q, n], agr.at[q, n], device_id=peer, device_id_type=MESH
        )

    far, near = 1 - zl, zl

    def core_flow(n, piece):
        half = (far, near)[n]
        return pltpu.make_async_remote_copy(
            GI.at[half * 2 + (1 - k), :, piece], D2D.at[half, :, piece],
            ds.at[n, piece], dr.at[n, piece], device_id=d_core, device_id_type=MESH,
        )

    def zl_flow(n, piece):
        at = pl.ds(2 * n, 2)
        return pltpu.make_async_remote_copy(
            SB.at[at, piece], RB.at[at, piece], zs.at[n, piece], zr.at[n, piece],
            device_id=d_zl, device_id_type=MESH,
        )

    def forward_x(q, piece=None):
        flow(3, q, piece).start()
        flow(4, q, piece).start()

    def forward_z(q, piece=None):
        flow(5, q, piece).start()
        flow(6, q, piece).start()

    def onward_x(q, piece=None):
        arrived(5, q, piece)
        flow(9, q, piece).start()
        arrived(6, q, piece)
        flow(10, q, piece).start()

    def onward_z(q):
        arrived(3, q)
        flow(7, q).start()
        arrived(4, q)
        flow(8, q).start()

    def turn_acts(slot):
        AT[:, pl.ds(pl.multiple_of(slot * 512, 512), 512)] = ACT[slot].T

    def input_sums(q, first, count, piece=None):
        rows = 512 if piece is None else 256

        @pl.loop(first, first + count)
        def _(j):
            o = jnp.where(j < 2, far, near) * 2 + jnp.where(lax.rem(j, 2) == 0, 1 - k, k)
            slots = pl.ds(o * 2, 2)
            if piece is None:
                parts = [G[q * GROUP + n, slots] for n in range(GROUP)]
            else:
                parts = [G[q * GROUP + n, slots, :, piece] for n in range(GROUP)]
            g = jnp.concatenate([p.reshape(rows, STRIP) for p in parts], axis=1)
            out = lax.dot_general(
                g, W[:, cols(q)], (((1,), (1,)), ((), ())), preferred_element_type=F32
            )
            if piece is None:
                GI[o] += out.reshape(4, 2, 64, 640)
            else:
                GI[o, :, piece] += out.reshape(4, 64, 640)

    def weight_grad(q):
        g = jnp.concatenate([G[q * GROUP + n].reshape(2048, STRIP) for n in range(GROUP)], axis=1)

        @pl.loop(0, 4)
        def _(p):
            rows = AT[pl.ds(pl.multiple_of(p * 160, 160), 160), :]
            out = jnp.dot(rows, g, preferred_element_type=F32).astype(BF16)
            for n in range(GROUP):
                GS[q * GROUP + n, p] = out[:, n * STRIP:(n + 1) * STRIP]

    def send_pieces(q):
        for n in range(4):
            rs_flow(n, q).start()

    def join_pieces(q):
        rs_flow(0, q).wait_recv()
        rs_flow(1, q).wait_recv()

        @pl.loop(q * GROUP, (q + 1) * GROUP)
        def _(s):
            GS[s, dup, TOP] = (GS[s, dup, TOP].astype(F32) + RS[s, 2, TOP].astype(F32)).astype(BF16)
            GS[s, ddn, LOW] = (GS[s, ddn, LOW].astype(F32) + RS[s, 2, LOW].astype(F32)).astype(BF16)

        rs_flow(4, q).start()
        rs_flow(5, q).start()

    def update(q):
        for n in range(2, 6):
            rs_flow(n, q).wait_recv()
        @pl.loop(q * GROUP, (q + 1) * GROUP)
        def _(s):
            grad = GS[s, d].astype(F32) + RS[s, 0].astype(F32) + RS[s, 1].astype(F32)
            at = pl.ds(pl.multiple_of(s * STRIP, STRIP), STRIP)
            a, b, e = adamw(grad * scale, new_master[:, at], new_one[:, at], new_two[:, at])
            new_weight[pl.ds(pl.multiple_of(d * 160, 160), 160), at] = a.astype(BF16)
            new_master[:, at] = a
            new_one[:, at] = b
            new_two[:, at] = e
        ag_flow(0, q).start()
        ag_flow(1, q).start()

    def forward_w(q):
        ag_flow(0, q).wait_recv()
        ag_flow(2, q).start()
        ag_flow(1, q).wait_recv()
        ag_flow(3, q).start()

    def own_x(q):
        flow(0, q).start()
        flow(1, q).start()

    for q in range(2):
        loaded_g(q)
        flow(2, q).start()
        own_x(q)
    load_a.wait()
    act_flow(0).start()
    act_flow(1).start()
    for q in (2, 3):
        loaded_g(q)
        flow(2, q).start()

    GI[...] = jnp.zeros_like(GI)
    turn_acts(col)
    def x_arrived(q):
        arrived(0, q)
        arrived(1, q)

    def z_arrived(q):
        arrived(2, q)

    def by_x(q):
        return q < BY_X

    x_arrived(0)
    forward_x(0)
    z_arrived(0)
    forward_z(0)
    act_flow(1).wait_recv()
    turn_acts(zl * 2 + (1 - k))
    x_arrived(1)
    forward_x(1)
    z_arrived(1)
    forward_z(1)
    if BY_X > 0:
        onward_x(0)
    own_x(2)
    load_w.wait()
    for n in range(3):
        load_o(n).wait()

    @pl.loop(2, nc)
    def _(i):
        q = i - 2

        @pl.when(i == 2)
        def _():
            act_flow(0).wait_recv()
            act_flow(2).start()
            turn_acts((1 - zl) * 2 + k)
            if BY_X > 1:
                onward_x(1)

        @pl.when((i > 2) & (i < last))
        def _():
            z_arrived(i)
            forward_z(i)

        @pl.when(i == last)
        def _():
            z_arrived(last)
            forward_z(last, 0)

        @pl.when(i - 1 >= max(BY_X, 1))
        def _():
            onward_z(i - 1)

        @pl.when(i >= 3)
        def _():
            join_pieces(i - 3)

        @pl.when(i == 2)
        def _():
            act_flow(2).wait_recv()
            turn_acts((1 - zl) * 2 + (1 - k))
        @pl.when(by_x(q))
        def _():
            arrived(3, q)
            arrived(4, q)

        @pl.when(jnp.logical_not(by_x(q)))
        def _():
            arrived(5, q)
            arrived(6, q)

        arrived(7, q)
        arrived(8, q)
        input_sums(q, 0, 4)

        @pl.when(i == 2)
        def _():
            z_arrived(2)
            forward_z(2)

        x_arrived(i)

        @pl.when(i < last)
        def _():
            forward_x(i)
            own_x(i + 1)

        @pl.when(i == last)
        def _():
            forward_x(last, 0)
            forward_z(last, 1)
            forward_x(last, 1)

        @pl.when(i + 2 < nc)
        def _():
            loaded_g(i + 2)
            flow(2, i + 2).start()

        @pl.when(i >= 4)
        def _():
            forward_w(i - 4)
        weight_grad(q)
        send_pieces(q)

        @pl.when(i >= 3)
        def _():
            update(i - 3)

    def far_sums(piece):
        core_flow(0, piece).wait_recv()
        for n in range(2):
            at = pl.ds(2 * n, 2)
            SB[at, piece] = (GI[far * 2 + k, at, piece] + D2D[far, at, piece]).astype(BF16)

    onward_x(last, 0)
    for n in (5, 6, 7, 8):
        arrived(n, last - 1)
    input_sums(last - 1, 0, 4)
    onward_x(last, 1)
    weight_grad(last - 1)
    send_pieces(last - 1)
    join_pieces(last - 2)

    for piece in range(2):
        for n in (3, 4, 7, 8):
            arrived(n, last, piece)
        input_sums(last, 0, 2, piece)
        if piece == 0:
            core_flow(0, 0).start()
        input_sums(last, 2, 2, piece)
        if piece == 0:
            core_flow(1, 0).start()
            forward_w(last - 3)
    core_flow(0, 1).start()
    far_sums(0)
    core_flow(1, 1).start()
    zl_flow(0, 0).start()
    zl_flow(1, 0).start()
    weight_grad(last)
    send_pieces(last)
    far_sums(1)
    join_pieces(last - 1)
    zl_flow(0, 1).start()
    zl_flow(1, 1).start()
    update(last - 2)
    join_pieces(last)
    update(last - 1)
    forward_w(last - 2)
    update(last)
    forward_w(last - 1)
    forward_w(last)
    @pl.loop(0, nc)
    def _(q):
        ag_flow(2, q).wait_recv()
        ag_flow(3, q).wait_recv()
    for piece in range(2):
        core_flow(1, piece).wait_recv()
        for n in range(2):
            zl_flow(n, piece).wait_recv()
            at = pl.ds(2 * n, 2)
            total = GI[col, at, piece] + D2D[near, at, piece] + RB[at, piece].astype(F32)
            grad_in[at, piece] = total.astype(BF16)

    @pl.loop(0, nc)
    def _(q):
        for m in range(3):
            flow(m, q).wait_send()
        for m in range(6):
            rs_flow(m, q).wait_send()
        for m in range(4):
            ag_flow(m, q).wait_send()

    @pl.loop(0, last)
    def _(q):
        for m in range(3, 9):
            flow(m, q).wait_send()

    for piece in range(2):
        for m in range(3, 9):
            flow(m, last, piece).wait_send()
        for n in range(2):
            core_flow(n, piece).wait_send()
            zl_flow(n, piece).wait_send()

    for n in range(3):
        act_flow(n).wait_send()


def write_out(*refs):
    held, outs, sems = refs[:5], refs[5:10], refs[10]
    copies = [pltpu.make_async_copy(a, b, sems.at[n]) for n, (a, b) in enumerate(zip(held, outs))]
    for copy in copies:
        copy.start()
    for copy in copies:
        copy.wait()


def per_device(acts, grad_out, weight, master, moment_one, moment_two):
    tokens_total = acts.shape[0] * lax.axis_size("col") * lax.axis_size("depth")
    width = grad_out.shape[1]
    strips = width // STRIP
    nc = strips // GROUP
    scale = float(1.0 / math.sqrt(tokens_total))
    dma = pltpu.SemaphoreType.DMA
    anywhere = pl.BlockSpec(memory_space=pl.ANY)
    on_chip = pl.BlockSpec(memory_space=pltpu.VMEM)

    def body(*refs):
        kernel(nc, scale, *refs)

    results = [((4, 2, 64, 640), BF16), (weight.shape, BF16)] + [(master.shape, F32)] * 3
    held = pl.pallas_call(
        body,
        out_shape=tuple(pltpu.VMEM(*r) for r in results),
        in_specs=[anywhere] * 6,
        out_specs=(on_chip,) * 5,
        scratch_shapes=[
            pltpu.VMEM((strips, 8, 2, 2, 64, STRIP), BF16),
            pltpu.VMEM((640, width), BF16),
            pltpu.VMEM((4, 512, 640), BF16),
            pltpu.VMEM((640, 2048), BF16),
            pltpu.VMEM((4, 4, 2, 64, 640), F32),
            pltpu.VMEM((2, 4, 2, 64, 640), F32),
            pltpu.VMEM((4, 2, 64, 640), BF16),
            pltpu.VMEM((4, 2, 64, 640), BF16),
            pltpu.VMEM((strips, 4, 160, STRIP), BF16),
            pltpu.VMEM((strips, 3, 160, STRIP), BF16),
            dma((nc, GROUP)), dma((1,)), dma((1,)), dma((3,)),
            dma((nc + 1, 9)), dma((nc + 1, 9)),
            dma((3,)), dma((3,)),
            dma((nc, 6)), dma((nc, 6)),
            dma((nc, 4)), dma((nc, 4)),
            dma((2, 2)), dma((2, 2)),
            dma((2, 2)), dma((2, 2)),
        ],
        compiler_params=pltpu.CompilerParams(
            collective_id=0, has_side_effects=True, vmem_limit_bytes=46 * 2**20
        ),
        name="step",
    )(acts, grad_out.reshape(2, 2, 64, width), weight, master, moment_one, moment_two)
    outs = pl.pallas_call(
        write_out,
        out_shape=tuple(jax.ShapeDtypeStruct(*r) for r in results),
        in_specs=[on_chip] * 5,
        out_specs=(anywhere,) * 5,
        scratch_shapes=[dma((5,))],
        compiler_params=pltpu.CompilerParams(vmem_limit_bytes=2**20),
        name="write_out",
    )(*[pltpu.with_memory_space_constraint(a, pltpu.VMEM) for a in held])
    return (outs[0].reshape(acts.shape), *outs[1:])


def solution(mesh):
    placed = (
        P(("depth", "col"), "row"),
        P(("depth", "row"), "col"),
        P("row", "col"),
        P(("row", "depth"), "col"),
        P(("row", "depth"), "col"),
        P(("row", "depth"), "col"),
    )
    return jax.shard_map(
        per_device,
        mesh=mesh,
        in_specs=placed,
        out_specs=(
            P(("depth", "col"), "row"),
            P("row", "col"),
            P(("row", "depth"), "col"),
            P(("row", "depth"), "col"),
            P(("row", "depth"), "col"),
        ),
        check_vma=False,
    )
```

time: 353 us -> 146 us (0.41)
  waiting for transfers between devices: 180 us -> 0 us
  Pallas kernels: 0 us -> 144 us
  blocking collectives: 113 us -> 0 us
  matrix products: 30.3 us -> 0 us
  between operations: 13.8 us -> 0.64 us
  other arithmetic: 10.8 us -> 0 us
  local copies, waits for them, and re-layouts: 5.15 us -> 0 us
    pallas_call x0 -> x2, Pallas kernels: none -> 144 us  [the longest x1 140 us: per_device(): pl.pallas_call(body, out_shape=tuple((pltpu.VMEM(*r) for r in results)),...]
    all_gather x2 -> x0, waiting for transfers between devices: 132 us -> none  [the longest x1 132 us: per_device(): whole_cotangent = lax.all_gather(grad_out, 'row', axis=0, tiled=True)]
    all_to_all x2 -> x0, blocking collectives: 113 us -> none  [the longest x1 62.6 us: sum_at_owner(): lax.all_to_all(parts, axis, split_axis=0, concat_axis=0, tiled=True)]
    reduce_scatter x1 -> x0, waiting for transfers between devices: 47.2 us -> none  [per_device(): lax.psum_scatter(lax.dot_general(picked, whole_cotangent, (((0,), (0,)),...]
    dot_general x2 -> x0, matrix products: 30.3 us -> none  [the longest x1 15.9 us: per_device(): lax.dot_general(picked, weight, (((1,), (1,)), ((), ())), preferred_eleme...]
    convert_element_type x1 -> x0, other arithmetic: 7.03 us -> none  [per_device(): new_master.astype(jnp.bfloat16)]
    unnamed x5 -> x0, local copies, waits for them, and re-layouts: 4.95 us -> none
    reduce_sum x1 -> x0, other arithmetic: 3.81 us -> none  [sum_at_owner(): return arrived.sum(axis=0)]
  transfers between devices with their start and end apart: 3 -> 0, of which waited for: 2 -> 0; matrix products, arithmetic and copies ran while one was open for 6% -> 0% of each run, Pallas kernels for 0% -> 0%
where the time goes in v2:
time: 146 us; the launch traced here: 145 us
  Pallas kernels  144 us (99%)
    pallas_call x1, Pallas kernels, per_device(): pl.pallas_call(body, out_shape=tuple((pltpu.VMEM(*r) for r in results)),...  140 us
    pallas_call x1, Pallas kernels, per_device(): pl.pallas_call(write_out, out_shape=tuple((jax.ShapeDtypeStruct(*r) for r...  4.4 us

profile of v2, /device:TPU:1, one launch (start us, length us, event | category | flops | bytes accessed | tf_op | source)
XLA Modules:
  0.0 144.6 jit_solution(3745813241766456254)
XLA Ops:
  0.6 139.5 %step.1 = (bf16[4,2,64,640]{3,2,1,0:T(8,128)(2,1)S(1)}, bf16[640,3456]{1,0:T(8,128)(2,1)S(1)}, f32[160,3456]{1,0:T(8,128)S(1)}, f32[160,3456]{1,0:T(8,128)S(1)}, f32[160,3456]{1,0:T(8,128)S(1)}) custom-call(bf16[512,640]{1,0:T(8,128)(2,1)} %refs_0_.1, bf16[2,2,64,3456]{3,2,1,0:T(8,128)(2,1)} %bitcast.2, bf16[640,3456]{1,0:T(8,128)(2,1)} %refs_2_.1, ...), custom_call_target="tpu_custom_call" | custom-call | tf_op jit(solution)/shard_map/step/pallas_call | solution.py:496
  140.2 4.4 %write_out.1 = (bf16[4,2,64,640]{3,2,1,0:T(8,128)(2,1)}, bf16[640,3456]{1,0:T(8,128)(2,1)}, f32[160,3456]{1,0:T(8,128)}, f32[160,3456]{1,0:T(8,128)}, f32[160,3456]{1,0:T(8,128)}) custom-call(bf16[4,2,64,640]{3,2,1,0:T(8,128)(2,1)S(1)} %get-tuple-element.15.refs_0_, bf16[640,3456]{1,0:T(8,128)(2,1)S(1)} %get-tuple-element.16.refs_1_, ...), custom_call_target="tpu_custom_call" | custom-call | tf_op jit(solution)/shard_map/write_out/pallas_call | solution.py:525

commit v3 on v2

--- a/solution.py
+++ b/solution.py
@@ -8,11 +8,14 @@
 from jax.sharding import PartitionSpec as P
 
 STEP = 10
-BY_X = 2
+PARTS = 2
+BY_X = 1
 STRIP = 128
-GROUP = 3
+GROUP = 2
+LAST = 3
+FIRST = 3
+AHEAD = 2
 WIDE = STRIP * GROUP
-
 MESH = pl.DeviceIdType.MESH
 F32, BF16 = jnp.float32, jnp.bfloat16
 
@@ -57,11 +60,14 @@
 
     last = nc - 1
 
+    def size(q):
+        return LAST if isinstance(q, int) and q == last else GROUP
+
     def strips(q):
-        return pl.ds(q * GROUP, GROUP)
+        return pl.ds(q * GROUP, size(q))
 
     def cols(q):
-        return pl.ds(pl.multiple_of(q * WIDE, STRIP), WIDE)
+        return pl.ds(pl.multiple_of(q * WIDE, STRIP), size(q) * STRIP)
 
     def load_g(q):
         return [
@@ -70,7 +76,7 @@
                 G.at[q * GROUP + n, me],
                 g_sem.at[q, n],
             )
-            for n in range(GROUP)
+            for n in range(size(q))
         ]
 
     def load_o(n):
@@ -96,10 +102,11 @@
     for peer in (d_right, d_left, d_zp, d_core, d_zl, d_up, d_dn):
         pl.semaphore_signal(barrier, inc=1, device_id=peer, device_id_type=MESH)
 
-    @pl.loop(2, nc)
+    @pl.loop(2, last)
     def _(q):
         start_g(q)
 
+    start_g(last)
     load_w.start()
     for n in range(3):
         load_o(n).start()
@@ -150,10 +157,11 @@
         )
 
     def ag_flow(n, q):
-        piece, first, count, peer = (
-            (d, 0, 160, d_up), (d, 0, 160, d_dn), (ddn, 0, 80, d_up), (dup, 80, 80, d_dn),
+        piece, first, peer = (
+            (d, 0, d_up), (d, 80, d_dn), (d, 80, d_up), (d, 0, d_dn),
+            (ddn, 0, d_up), (dup, 80, d_dn),
         )[n]
-        rows = pl.ds(pl.multiple_of(piece * 160 + first, 16), count)
+        rows = pl.ds(pl.multiple_of(piece * 160 + first, 16), 80)
         ref = new_weight.at[rows, cols(q)]
         return pltpu.make_async_remote_copy(
             ref, ref, ags.at[q, n], agr.at[q, n], device_id=peer, device_id_type=MESH
@@ -198,6 +206,9 @@
     def turn_acts(slot):
         AT[:, pl.ds(pl.multiple_of(slot * 512, 512), 512)] = ACT[slot].T
 
+    def side_by_side(parts):
+        return parts[0] if len(parts) == 1 else jnp.concatenate(parts, axis=1)
+
     def input_sums(q, first, count, piece=None):
         rows = 512 if piece is None else 256
 
@@ -206,10 +217,10 @@
             o = jnp.where(j < 2, far, near) * 2 + jnp.where(lax.rem(j, 2) == 0, 1 - k, k)
             slots = pl.ds(o * 2, 2)
             if piece is None:
-                parts = [G[q * GROUP + n, slots] for n in range(GROUP)]
+                parts = [G[q * GROUP + n, slots] for n in range(size(q))]
             else:
-                parts = [G[q * GROUP + n, slots, :, piece] for n in range(GROUP)]
-            g = jnp.concatenate([p.reshape(rows, STRIP) for p in parts], axis=1)
+                parts = [G[q * GROUP + n, slots, :, piece] for n in range(size(q))]
+            g = side_by_side([p.reshape(rows, STRIP) for p in parts])
             out = lax.dot_general(
                 g, W[:, cols(q)], (((1,), (1,)), ((), ())), preferred_element_type=F32
             )
@@ -219,13 +230,13 @@
                 GI[o, :, piece] += out.reshape(4, 64, 640)
 
     def weight_grad(q):
-        g = jnp.concatenate([G[q * GROUP + n].reshape(2048, STRIP) for n in range(GROUP)], axis=1)
+        g = side_by_side([G[q * GROUP + n].reshape(2048, STRIP) for n in range(size(q))])
 
         @pl.loop(0, 4)
         def _(p):
             rows = AT[pl.ds(pl.multiple_of(p * 160, 160), 160), :]
             out = jnp.dot(rows, g, preferred_element_type=F32).astype(BF16)
-            for n in range(GROUP):
+            for n in range(size(q)):
                 GS[q * GROUP + n, p] = out[:, n * STRIP:(n + 1) * STRIP]
 
     def send_pieces(q):
@@ -236,7 +247,7 @@
         rs_flow(0, q).wait_recv()
         rs_flow(1, q).wait_recv()
 
-        @pl.loop(q * GROUP, (q + 1) * GROUP)
+        @pl.loop(q * GROUP, q * GROUP + size(q))
         def _(s):
             GS[s, dup, TOP] = (GS[s, dup, TOP].astype(F32) + RS[s, 2, TOP].astype(F32)).astype(BF16)
             GS[s, ddn, LOW] = (GS[s, ddn, LOW].astype(F32) + RS[s, 2, LOW].astype(F32)).astype(BF16)
@@ -247,7 +258,7 @@
     def update(q):
         for n in range(2, 6):
             rs_flow(n, q).wait_recv()
-        @pl.loop(q * GROUP, (q + 1) * GROUP)
+        @pl.loop(q * GROUP, q * GROUP + size(q))
         def _(s):
             grad = GS[s, d].astype(F32) + RS[s, 0].astype(F32) + RS[s, 1].astype(F32)
             at = pl.ds(pl.multiple_of(s * STRIP, STRIP), STRIP)
@@ -256,14 +267,14 @@
             new_master[:, at] = a
             new_one[:, at] = b
             new_two[:, at] = e
-        ag_flow(0, q).start()
-        ag_flow(1, q).start()
+        for n in range(4):
+            ag_flow(n, q).start()
 
     def forward_w(q):
         ag_flow(0, q).wait_recv()
-        ag_flow(2, q).start()
+        ag_flow(4, q).start()
         ag_flow(1, q).wait_recv()
-        ag_flow(3, q).start()
+        ag_flow(5, q).start()
 
     def own_x(q):
         flow(0, q).start()
@@ -273,10 +284,13 @@
         loaded_g(q)
         flow(2, q).start()
         own_x(q)
+    if FIRST > 2:
+        loaded_g(2)
+        flow(2, 2).start()
     load_a.wait()
     act_flow(0).start()
     act_flow(1).start()
-    for q in (2, 3):
+    for q in range(FIRST, FIRST + 2):
         loaded_g(q)
         flow(2, q).start()
 
@@ -292,101 +306,143 @@
     def by_x(q):
         return q < BY_X
 
+    def compute(q, between):
+        if isinstance(q, int):
+            skip = (3, 4) if q < BY_X else (5, 6)
+            arrived(skip[0], q)
+            arrived(skip[1], q)
+        else:
+            @pl.when(q < BY_X)
+            def _():
+                arrived(3, q)
+                arrived(4, q)
+
+            @pl.when(q >= BY_X)
+            def _():
+                arrived(5, q)
+                arrived(6, q)
+
+        arrived(7, q)
+        arrived(8, q)
+        input_sums(q, 0, 4)
+        between()
+        weight_grad(q)
+        send_pieces(q)
+
+    def onward(q):
+        onward_x(q) if q < BY_X else onward_z(q)
+
     x_arrived(0)
     forward_x(0)
     z_arrived(0)
     forward_z(0)
+    if AHEAD > 1:
+        own_x(2)
     act_flow(1).wait_recv()
     turn_acts(zl * 2 + (1 - k))
     x_arrived(1)
     forward_x(1)
     z_arrived(1)
     forward_z(1)
-    if BY_X > 0:
-        onward_x(0)
-    own_x(2)
+    onward(0)
+    own_x(2) if AHEAD < 2 else own_x(3)
+    if FIRST > 2:
+        z_arrived(2)
+        forward_z(2)
+        onward(1)
+        loaded_g(FIRST + 2)
+        flow(2, FIRST + 2).start()
+        x_arrived(2)
+        forward_x(2)
+        own_x(2 + AHEAD)
     load_w.wait()
     for n in range(3):
         load_o(n).wait()
-
-    @pl.loop(2, nc)
+    act_flow(0).wait_recv()
+    act_flow(2).start()
+    turn_acts((1 - zl) * 2 + k)
+    onward(FIRST - 1)
+    act_flow(2).wait_recv()
+    turn_acts((1 - zl) * 2 + (1 - k))
+    def forward_first():
+        z_arrived(FIRST)
+        forward_z(FIRST)
+        x_arrived(FIRST)
+        forward_x(FIRST)
+        own_x(FIRST + AHEAD)
+
+    compute(0, forward_first)
+
+    @pl.loop(FIRST, nc)
     def _(i):
-        q = i - 2
-
-        @pl.when(i == 2)
-        def _():
-            act_flow(0).wait_recv()
-            act_flow(2).start()
-            turn_acts((1 - zl) * 2 + k)
-            if BY_X > 1:
-                onward_x(1)
-
-        @pl.when((i > 2) & (i < last))
-        def _():
-            z_arrived(i)
-            forward_z(i)
-
-        @pl.when(i == last)
-        def _():
-            z_arrived(last)
-            forward_z(last, 0)
-
-        @pl.when(i - 1 >= max(BY_X, 1))
+        @pl.when(i > FIRST)
         def _():
             onward_z(i - 1)
 
-        @pl.when(i >= 3)
+        @pl.when(i > FIRST)
         def _():
             join_pieces(i - 3)
 
-        @pl.when(i == 2)
+        @pl.when(i == FIRST + 1)
         def _():
-            act_flow(2).wait_recv()
-            turn_acts((1 - zl) * 2 + (1 - k))
-        @pl.when(by_x(q))
-        def _():
-            arrived(3, q)
-            arrived(4, q)
-
-        @pl.when(jnp.logical_not(by_x(q)))
-        def _():
-            arrived(5, q)
-            arrived(6, q)
-
-        arrived(7, q)
-        arrived(8, q)
-        input_sums(q, 0, 4)
-
-        @pl.when(i == 2)
-        def _():
-            z_arrived(2)
-            forward_z(2)
-
-        x_arrived(i)
-
-        @pl.when(i < last)
-        def _():
-            forward_x(i)
-            own_x(i + 1)
-
-        @pl.when(i == last)
-        def _():
-            forward_x(last, 0)
-            forward_z(last, 1)
-            forward_x(last, 1)
-
-        @pl.when(i + 2 < nc)
-        def _():
-            loaded_g(i + 2)
-            flow(2, i + 2).start()
-
-        @pl.when(i >= 4)
-        def _():
-            forward_w(i - 4)
-        weight_grad(q)
-        send_pieces(q)
-
-        @pl.when(i >= 3)
+            update(0)
+
+        def between():
+            @pl.when((i > FIRST) & (i < last))
+            def _():
+                x_arrived(i)
+                forward_x(i)
+
+            @pl.when((i > FIRST) & (i + AHEAD < last))
+            def _():
+                own_x(i + AHEAD)
+
+            @pl.when(i + AHEAD == last)
+            def _():
+                own_x(last)
+
+            @pl.when(i + 1 < last)
+            def _():
+                z_arrived(i + 1)
+                forward_z(i + 1)
+
+            @pl.when(i + 1 == last)
+            def _():
+                z_arrived(last)
+                forward_z(last, 0)
+
+            @pl.when(i == last)
+            def _():
+                x_arrived(last)
+                forward_x(last, 0)
+                forward_z(last, 1)
+                forward_x(last, 1)
+
+            @pl.when(i + 3 < last)
+            def _():
+                loaded_g(i + 3)
+                flow(2, i + 3).start()
+
+            @pl.when(i + 3 == last)
+            def _():
+                loaded_g(last)
+                flow(2, last).start()
+
+            @pl.when(i == FIRST)
+            def _():
+                join_pieces(0)
+
+            @pl.when(i == FIRST + 2)
+            def _():
+                forward_w(0)
+
+            @pl.when(i >= FIRST + 2)
+            def _():
+                forward_w(i - 4)
+
+        compute(i - 2, between)
+
+        @pl.when(i > FIRST)
         def _():
             update(i - 3)
 
@@ -397,46 +453,44 @@
             SB[at, piece] = (GI[far * 2 + k, at, piece] + D2D[far, at, piece]).astype(BF16)
 
     onward_x(last, 0)
-    for n in (5, 6, 7, 8):
-        arrived(n, last - 1)
-    input_sums(last - 1, 0, 4)
-    onward_x(last, 1)
-    weight_grad(last - 1)
-    send_pieces(last - 1)
+    compute(last - 1, lambda: onward_x(last, 1))
     join_pieces(last - 2)
 
-    for piece in range(2):
-        for n in (3, 4, 7, 8):
-            arrived(n, last, piece)
+    def last_sums(piece):
         input_sums(last, 0, 2, piece)
-        if piece == 0:
-            core_flow(0, 0).start()
+        core_flow(0, piece).start()
         input_sums(last, 2, 2, piece)
-        if piece == 0:
-            core_flow(1, 0).start()
-            forward_w(last - 3)
-    core_flow(0, 1).start()
+        core_flow(1, piece).start()
+    for n in (3, 4, 7, 8):
+        arrived(n, last, 0)
+    last_sums(0)
+    forward_w(last - 3)
+    for n in (3, 4, 7, 8):
+        arrived(n, last, 1)
+    weight_grad(last)
     far_sums(0)
-    core_flow(1, 1).start()
+    send_pieces(last)
     zl_flow(0, 0).start()
     zl_flow(1, 0).start()
-    weight_grad(last)
-    send_pieces(last)
+    last_sums(1)
+    join_pieces(last - 1)
     far_sums(1)
-    join_pieces(last - 1)
+    update(last - 2)
     zl_flow(0, 1).start()
     zl_flow(1, 1).start()
-    update(last - 2)
     join_pieces(last)
     update(last - 1)
     forward_w(last - 2)
     update(last)
     forward_w(last - 1)
     forward_w(last)
-    @pl.loop(0, nc)
+    @pl.loop(0, last)
     def _(q):
-        ag_flow(2, q).wait_recv()
-        ag_flow(3, q).wait_recv()
+        for n in range(2, 6):
+            ag_flow(n, q).wait_recv()
+
+    for n in range(2, 6):
+        ag_flow(n, last).wait_recv()
     for piece in range(2):
         core_flow(1, piece).wait_recv()
         for n in range(2):
@@ -445,20 +499,20 @@
             total = GI[col, at, piece] + D2D[near, at, piece] + RB[at, piece].astype(F32)
             grad_in[at, piece] = total.astype(BF16)
 
-    @pl.loop(0, nc)
-    def _(q):
+    def sent(q):
         for m in range(3):
             flow(m, q).wait_send()
         for m in range(6):
             rs_flow(m, q).wait_send()
-        for m in range(4):
             ag_flow(m, q).wait_send()
 
     @pl.loop(0, last)
     def _(q):
+        sent(q)
         for m in range(3, 9):
             flow(m, q).wait_send()
 
+    sent(last)
     for piece in range(2):
         for m in range(3, 9):
             flow(m, last, piece).wait_send()
@@ -472,7 +526,12 @@
 
 def write_out(*refs):
     held, outs, sems = refs[:5], refs[5:10], refs[10]
-    copies = [pltpu.make_async_copy(a, b, sems.at[n]) for n, (a, b) in enumerate(zip(held, outs))]
+    pairs = [(held[0], outs[0])]
+    for a, b in zip(held[1:], outs[1:]):
+        part = a.shape[0] // PARTS
+        rows = [pl.ds(n * part, part) for n in range(PARTS)]
+        pairs += [(a.at[r], b.at[r]) for r in rows]
+    copies = [pltpu.make_async_copy(a, b, sems.at[n]) for n, (a, b) in enumerate(pairs)]
     for copy in copies:
         copy.start()
     for copy in copies:
@@ -483,7 +542,7 @@
     tokens_total = acts.shape[0] * lax.axis_size("col") * lax.axis_size("depth")
     width = grad_out.shape[1]
     strips = width // STRIP
-    nc = strips // GROUP
+    nc = (strips - LAST) // GROUP + 1
     scale = float(1.0 / math.sqrt(tokens_total))
     dma = pltpu.SemaphoreType.DMA
     anywhere = pl.BlockSpec(memory_space=pl.ANY)
@@ -509,11 +568,11 @@
             pltpu.VMEM((4, 2, 64, 640), BF16),
             pltpu.VMEM((strips, 4, 160, STRIP), BF16),
             pltpu.VMEM((strips, 3, 160, STRIP), BF16),
-            dma((nc, GROUP)), dma((1,)), dma((1,)), dma((3,)),
+            dma((nc, max(GROUP, LAST))), dma((1,)), dma((1,)), dma((3,)),
             dma((nc + 1, 9)), dma((nc + 1, 9)),
             dma((3,)), dma((3,)),
             dma((nc, 6)), dma((nc, 6)),
-            dma((nc, 4)), dma((nc, 4)),
+            dma((nc, 6)), dma((nc, 6)),
             dma((2, 2)), dma((2, 2)),
             dma((2, 2)), dma((2, 2)),
         ],
@@ -527,7 +586,7 @@
         out_shape=tuple(jax.ShapeDtypeStruct(*r) for r in results),
         in_specs=[on_chip] * 5,
         out_specs=(anywhere,) * 5,
-        scratch_shapes=[dma((5,))],
+        scratch_shapes=[dma((1 + 4 * PARTS,))],
         compiler_params=pltpu.CompilerParams(vmem_limit_bytes=2**20),
         name="write_out",
     )(*[pltpu.with_memory_space_constraint(a, pltpu.VMEM) for a in held])

time: 146 us -> 143 us (0.979)
  Pallas kernels: 144 us -> 142 us
    pallas_call x1, Pallas kernels: 140 us -> 138 us  [per_device(): pl.pallas_call(body, out_shape=tuple((pltpu.VMEM(*r) for r in results)),...]
where the time goes in v3:
time: 143 us
  Pallas kernels  142 us (99%)
    pallas_call x1, Pallas kernels, per_device(): pl.pallas_call(body, out_shape=tuple((pltpu.VMEM(*r) for r in results)),...  138 us
    pallas_call x1, Pallas kernels, per_device(): pl.pallas_call(write_out, out_shape=tuple((jax.ShapeDtypeStruct(*r) for r...  4.4 us

profile of v3, /device:TPU:1, one launch (start us, length us, event | category | flops | bytes accessed | tf_op | source)
XLA Modules:
  0.0 142.6 jit_solution(11866224786013257547)
XLA Ops:
  0.6 137.5 %step.1 = (bf16[4,2,64,640]{3,2,1,0:T(8,128)(2,1)S(1)}, bf16[640,3456]{1,0:T(8,128)(2,1)S(1)}, f32[160,3456]{1,0:T(8,128)S(1)}, f32[160,3456]{1,0:T(8,128)S(1)}, f32[160,3456]{1,0:T(8,128)S(1)}) custom-call(bf16[512,640]{1,0:T(8,128)(2,1)} %refs_0_.1, bf16[2,2,64,3456]{3,2,1,0:T(8,128)(2,1)} %bitcast.2, bf16[640,3456]{1,0:T(8,128)(2,1)} %refs_2_.1, ...), custom_call_target="tpu_custom_call" | custom-call | tf_op jit(solution)/shard_map/step/pallas_call | solution.py:555
  138.2 4.4 %write_out.1 = (bf16[4,2,64,640]{3,2,1,0:T(8,128)(2,1)}, bf16[640,3456]{1,0:T(8,128)(2,1)}, f32[160,3456]{1,0:T(8,128)}, f32[160,3456]{1,0:T(8,128)}, f32[160,3456]{1,0:T(8,128)}) custom-call(bf16[4,2,64,640]{3,2,1,0:T(8,128)(2,1)S(1)} %get-tuple-element.15.refs_0_, bf16[640,3456]{1,0:T(8,128)(2,1)S(1)} %get-tuple-element.16.refs_1_, ...), custom_call_target="tpu_custom_call" | custom-call | tf_op jit(solution)/shard_map/write_out/pallas_call | solution.py:584
